TPU v7x, 128 devices: a whole 4x4x4 slice. The times are simulated.
128 devices in a mesh: gx: 4 (over x), gy: 4 (over z), gz: 8 (over y, core).
Axes of the slice: x: 4, y: 4, z: 4, core: 2. Of those that a mesh axis runs over, the one named last changes fastest.
Arguments:
- coords: float32 [4, 4, 24, 3, 128], P('gx', 'gy', 'gz'), as said below
- polar: float32 [4, 4, 24, 128], P('gx', 'gy', 'gz'), may hold values from 0.3 to 1.2
- field: float32 [4, 4, 24, 6, 128], P('gx', 'gy', 'gz'), may hold values from -6 to 6
- atom_count: int32 [4, 4, 24], P('gx', 'gy', 'gz'), may hold values from 64 to 128, as said below
- pair_list: int32 [4, 4, 24, 13], P('gx', 'gy', 'gz'), may hold values from -1 to 26, as said below
Outputs:
- dipoles: float32 [4, 4, 24, 6, 128], P('gx', 'gy', 'gz')
- residual: float32 [4, 4, 24, 6, 128], P('gx', 'gy', 'gz')
Inputs may be any that keep to these rules, and one draw needn't show every extreme that they name: `coords`: each coordinate lies within a quarter of 2.2 of its lattice site: atom slot a sits at 2.2 (a % 4 + 0.5, (a // 4) % 4 + 0.5, a // 16 + 0.5). `atom_count`: some block holds 128 atoms. `pair_list`: each block's row holds distinct codes above 13 in ascending order, followed by -1 in the unused entries.
All inputs are finite; a program needn't handle non-finite values.
Results may differ from a plain program's by a relative error of at most 0.0003.
Values sent between devices are 32-bit elements; how exact they have to be, the bound alone decides.
A program may use at most 64 MiB of HBM per device.

v0:
```python
import functools

import jax
import jax.numpy as jnp
from jax import lax
from jax.experimental import pallas as pl
from jax.experimental.pallas import tpu as pltpu
from jax.sharding import PartitionSpec as P


F32 = jnp.float32
I32 = jnp.int32
MESH = pl.DeviceIdType.MESH
SPACING = 2.2
HIGH = 2.1875
LOW = 0.0125
CUT2 = 49.0
THOLE = 0.39
SIZES = {"gx": 4, "gy": 4, "gz": 8}

NEAR = [(ox, oy, oz) for ox in (-1, 0, 1) for oy in (-1, 0, 1) for oz in (-1, 0, 1) if (ox, oy, oz) != (0, 0, 0)]
NEAR_ID = {n: i for i, n in enumerate(NEAR)}
FLAT = [n for n in NEAR if n[2] == 0]
FLAT_ID = {n: i for i, n in enumerate(FLAT)}
EDGE = [n for n in NEAR if n[2] != 0]
EDGE_ID = {n: i for i, n in enumerate(EDGE)}
PLANE = [(i, j) for i in range(4) for j in range(4)]
GREETED = sorted(
    {(ox % 4, oy % 4, oz % 8) for ox, oy, oz in NEAR}
    | {(i, j, 0) for i, j in PLANE if (i, j) != (0, 0)}
    | {(0, 0, k) for k in range(1, 8)}
)

OWN_COLS = [3, 4, 5, 6]
FAR_COLS = [0, 1, 2, 7, 8, 9]
OWN_PAIRS = [(x, c) for c in OWN_COLS for x in range(4)]
FAR_PAIRS = [(x, c) for c in FAR_COLS for x in range(4) if abs(c - 3 - x) <= 3]


def col_home(col):
    return (-1, col + 1) if col < 3 else (0, col - 3) if col < 7 else (1, col - 7)


def lanes():
    return lax.broadcasted_iota(I32, (8, 128), 1)


def subs():
    return lax.broadcasted_iota(I32, (8, 128), 0)


def row_of(ref, *where):
    return jnp.broadcast_to(ref[where], (8, 128))


def kernel(
    coords, polar, field, count, pairs, dip_out, res_out,
    packed, first, first_edge, vec, vec_edge, src, pol, ipol, own_geo,
    in_first, in_first_edge, in_vec, in_vec_edge, ext, merged, geo, act, dip, tens, acc, rows,
    part, in_plane, part2, in_line,
    send_sem, recv_sem, plane_send, plane_recv, line_send, line_recv,
):
    me = {a: lax.axis_index(a) for a in SIZES}

    def at(ox, oy, oz):
        off = {"gx": ox, "gy": oy, "gz": oz}
        return {a: lax.rem(me[a] + off[a] % SIZES[a], SIZES[a]) for a in SIZES}

    barrier = pltpu.get_barrier_semaphore()
    for ox, oy, oz in GREETED:
        pl.semaphore_signal(barrier, inc=1, device_id=at(ox, oy, oz), device_id_type=MESH)

    lane, sub = lanes(), subs()
    l32 = lane & 31
    zz = l32 - 3
    group = lane >> 5
    blk = zz >> 3
    valid = (zz >= 0) & (zz < 24)
    dz = 3 - sub

    for b in range(3):
        slot = lane
        mask = (slot[0:1] < count[0, 0, b]).astype(F32)
        packed[b, 0] = jnp.zeros((8, 128), F32)
        packed[b, 1] = jnp.zeros((8, 128), F32)
        packed[b, 0, 0:6, :] = field[0, 0, b] * mask
        pol_row = polar[0, 0, b : b + 1, :]
        packed[b, 0, 6:7, :] = pol_row
        s3 = slot[0:3]
        r3 = sub[0:3]
        site = jnp.where(r3 == 0, s3 & 3, jnp.where(r3 == 1, (s3 >> 2) & 3, s3 >> 4)).astype(F32) + 0.5
        packed[b, 1, 0:3, :] = (coords[0, 0, b] - site * HIGH) - site * LOW
        packed[b, 1, 3:4, :] = mask * lax.rsqrt(pol_row)
    bits = []
    for b in range(3):
        word = jnp.int32(0)
        for k in range(13):
            word = word | (jnp.int32(1) << (pairs[0, 0, b, k] & 31))
        bits.append(word)
    word = jnp.where(blk <= 0, bits[0], jnp.where(blk == 1, bits[1], bits[2]))
    for x in range(4):
        pick = 16 * (zz & 7) + 4 * group + x
        tile = []
        for t in range(2):
            got = [jnp.take_along_axis(packed[b, t], pick, axis=1) for b in range(3)]
            tile.append(jnp.where(valid, jnp.where(blk == 0, got[0], jnp.where(blk == 1, got[1], got[2])), 0.0))
        code = jnp.where(sub == 7, 14, jnp.maximum(15 + 3 * x + sub - 4, 0))
        flag = (lax.shift_right_logical(word, code) & 1).astype(F32)
        first[x, 0:8, :] = jnp.where((sub >= 4) & valid, flag, tile[1])
        src[x] = jnp.where(sub < 6, tile[0], 0.0)
        rows[x] = jnp.where((sub == 6) & valid, tile[0], 1.0)
        p = row_of(rows, x, slice(6, 7))
        pol[x] = p
        ipol[x] = 1.0 / p
        first[x, 8:16, :] = src[x] * p

    def edge_of(tiles):
        out = jnp.zeros((8, 128), F32)
        for x in range(4):
            top = pltpu.roll(tiles[x], (8 * x - 24) % 128, 1)
            low = pltpu.roll(tiles[x], (8 * x + 1) % 128, 1)
            out = jnp.where((l32 >= 8 * x) & (l32 < 8 * x + 3), top, out)
            out = jnp.where((l32 >= 8 * x + 4) & (l32 < 8 * x + 7), low, out)
        return out

    first_edge[0:8, :] = edge_of([first[x, 0:8, :] for x in range(4)])
    first_edge[8:16, :] = edge_of([first[x, 8:16, :] for x in range(4)])

    pl.semaphore_wait(barrier, len(GREETED))

    def copy(phase, n, incoming):
        ox, oy, oz = n if not incoming else tuple(-v for v in n)
        back = (-ox, -oy, -oz)
        count_rows = 14 if phase == 0 else 6
        if oz == 0:
            lo, hi = (1, 4) if ox == 1 else (0, 3) if ox == -1 else (0, 4)
            if phase == 0:
                s, d = first, in_first.at[FLAT_ID[back]]
            else:
                s, d = vec.at[phase - 1], in_vec.at[phase - 1, FLAT_ID[back]]
            s, d = s.at[lo:hi, 0:count_rows, :], d.at[lo:hi, 0:count_rows, :]
        else:
            if phase == 0:
                s, d = first_edge, in_first_edge.at[EDGE_ID[back]]
            else:
                s, d = vec_edge.at[phase - 1], in_vec_edge.at[phase - 1, EDGE_ID[back]]
            s, d = s.at[0:count_rows, :], d.at[0:count_rows, :]
        return pltpu.make_async_remote_copy(
            src_ref=s, dst_ref=d,
            send_sem=send_sem.at[phase, NEAR_ID[(ox, oy, oz)]], recv_sem=recv_sem.at[phase, NEAR_ID[back]],
            device_id=at(ox, oy, oz), device_id_type=MESH,
        )

    ORDER = sorted(NEAR, key=lambda n: (n[0] == 0, -sum(map(abs, n))))

    def send(phase):
        for n in sorted(NEAR, key=lambda n: (n[2] != 0, -sum(map(abs, n)))):
            copy(phase, n, False).start()

    def await_near(phase, far):
        for n in ORDER:
            if (n[0] != 0) == far:
                copy(phase, n, True).wait_recv()

    def ext_tile(phase, r0, ox, oy, x):
        if phase == 0:
            here = first[x, r0 : r0 + 8, :] if (ox, oy) == (0, 0) else in_first[FLAT_ID[(ox, oy, 0)], x, r0 : r0 + 8, :]
            low = in_first_edge[EDGE_ID[(ox, oy, -1)], r0 : r0 + 8, :]
            top = in_first_edge[EDGE_ID[(ox, oy, 1)], r0 : r0 + 8, :]
        else:
            here = vec[phase - 1, x] if (ox, oy) == (0, 0) else in_vec[phase - 1, FLAT_ID[(ox, oy, 0)], x]
            low = in_vec_edge[phase - 1, EDGE_ID[(ox, oy, -1)]]
            top = in_vec_edge[phase - 1, EDGE_ID[(ox, oy, 1)]]
        low = pltpu.roll(low, (-8 * x) % 128, 1)
        top = pltpu.roll(top, (23 - 8 * x) % 128, 1)
        return jnp.where(l32 < 3, low, jnp.where(l32 >= 27, top, here))

    def slide(ref, where, shift):
        return pltpu.roll(row_of(ref, *where), shift % 128, 1, stride=1, stride_axis=0)

    def merge_column(phase, r0, col):
        ox, x = col_home(col)
        tiles = {oy: ext_tile(phase, r0, ox, oy, x) for oy in (-1, 0, 1)}
        for k in range(7):
            dy = k - 3
            if dy > 0:
                tile = jnp.where(group < dy, tiles[1], tiles[0])
            elif dy < 0:
                tile = jnp.where(group >= 4 + dy, tiles[-1], tiles[0])
            else:
                tile = pltpu.roll(tiles[0], 64, 1)
            merged[col, k] = tile
        return tiles

    def merged_shift(k):
        return -32 * (k - 3) - 3 - (64 if k == 3 else 0)

    def spread_dipoles(phase, cols):
        for col in cols:
            merge_column(phase, 8 if phase == 0 else 0, col)
        for col in cols:
            for k in range(7):
                for c in range(6):
                    dip[col, k, c] = slide(merged, (col, k, slice(c, c + 1)), merged_shift(k))

    zp = zz + dz
    oz = (lax.shift_right_arithmetic(zp + 8, 3)) - (lax.shift_right_arithmetic(zz + 8, 3))
    lawful = valid & (sub < 7)

    def forward_act(ox, oy):
        x = 0 if ox == 0 else 2 + oy
        k = [row_of(first, x, slice(4 + i, 5 + i)) for i in range(3)]
        return jnp.where(oz == 0, k[1], jnp.where(oz > 0, k[2], k[0]))

    def backward_act(ox, oy):
        x = 0 if ox == 0 else 2 - oy
        ext[0] = ext_tile(0, 0, ox, oy, x)
        k = [slide(ext, (0, slice(4 + i, 5 + i)), -35) for i in range(3)]
        return jnp.where(oz == 0, k[1], jnp.where(oz > 0, k[0], k[2]))

    def self_act():
        ext[0] = ext_tile(0, 0, 0, 0, 0)
        up = row_of(first, 0, slice(7, 8))
        down = slide(ext, (0, slice(7, 8)), -35)
        return jnp.where(oz == 0, 1.0, jnp.where(oz > 0, up, down))

    def acts(ox):
        if ox == 0:
            a = {-1: backward_act(0, -1), 0: self_act(), 1: forward_act(0, 1)}
        else:
            a = {oy: (forward_act if ox > 0 else backward_act)(ox, oy) for oy in (-1, 0, 1)}
        for k in range(7):
            to = group + (k - 3)
            tile = jnp.where(to < 0, a[-1], jnp.where(to > 3, a[1], a[0]))
            act[ox + 1, k] = jnp.where(lawful, tile, 0.0)

    def spread_geometry(cols):
        for ox in sorted({col_home(c)[0] for c in cols}):
            acts(ox)
        for col in cols:
            merge_column(0, 0, col)
        for col in cols:
            ox, x = col_home(col)
            for k in range(7):
                for c in range(4):
                    tile = slide(merged, (col, k, slice(c, c + 1)), merged_shift(k))
                    if c == 2:
                        tile = tile + SPACING * dz.astype(F32)
                    if c == 3:
                        tile = tile * act[ox + 1, k]
                    geo[col, k, c] = tile

    def tensors(pair_list, base):
        def body(k, carry):
            shift_y = SPACING * (k - 3).astype(F32)
            for i, (x, col) in enumerate(pair_list):
                off_x = col - 3 - x
                dx = geo[col, k, 0] - own_geo[x, 0]
                if off_x:
                    dx = dx + SPACING * off_x
                dy = geo[col, k, 1] - own_geo[x, 1] + shift_y
                dzz = geo[col, k, 2] - own_geo[x, 2]
                strength = geo[col, k, 3] * own_geo[x, 3]
                if off_x == 0:
                    strength = jnp.where((sub == 3) & (k == 3), 0.0, strength)
                r2 = jnp.maximum(dx * dx + dy * dy + dzz * dzz, 1.0)
                ir = lax.rsqrt(r2)
                ir2 = ir * ir
                ir3 = ir * ir2
                u = r2 * (r2 * ir) * strength
                e = jnp.exp(-u)
                l3 = 1.0 - e
                l5 = l3 - u * e
                s = jnp.maximum(1.0 - r2 * (1.0 / CUT2), 0.0)
                si = s * s * ir3
                w3 = si * l3
                w5 = si * l5 * (3.0 * ir2)
                ax, ay, az = w5 * dx, w5 * dy, w5 * dzz
                tens[k, base + i, 0] = ax * dx - w3
                tens[k, base + i, 1] = ax * dy
                tens[k, base + i, 2] = ax * dzz
                tens[k, base + i, 3] = ay * dy - w3
                tens[k, base + i, 4] = ay * dzz
                tens[k, base + i, 5] = az * dzz - w3
            return carry

        lax.fori_loop(0, 7, body, 0)

    def apply(pair_list, base, start):
        used = sorted({x for x, _ in pair_list})

        def body(k, sums):
            sums = list(sums)
            for i, (x, col) in enumerate(pair_list):
                t = [tens[k, base + i, j] for j in range(6)]
                for s in range(2):
                    vx, vy, vz = (dip[col, k, 3 * s + j] for j in range(3))
                    o = 6 * x + 3 * s
                    sums[o] = sums[o] + (t[0] * vx + t[1] * vy + t[2] * vz)
                    sums[o + 1] = sums[o + 1] + (t[1] * vx + t[3] * vy + t[4] * vz)
                    sums[o + 2] = sums[o + 2] + (t[2] * vx + t[4] * vy + t[5] * vz)
            return tuple(sums)

        return lax.fori_loop(0, 7, body, start)

    def gather_field(phase):
        await_near(phase, False)
        if phase == 0:
            spread_geometry(OWN_COLS)
            tensors(OWN_PAIRS, 0)
        spread_dipoles(phase, OWN_COLS)
        sums = apply(OWN_PAIRS, 0, tuple(jnp.zeros((8, 128), F32) for _ in range(24)))
        for i in range(24):
            acc[i] = sums[i]
        await_near(phase, True)
        if phase == 0:
            spread_geometry(FAR_COLS)
            tensors(FAR_PAIRS, 16)
        spread_dipoles(phase, FAR_COLS)
        sums = apply(FAR_PAIRS, 16, tuple(acc[i] for i in range(24)))
        out = []
        for x in range(4):
            for c in range(6):
                rows[x, c : c + 1, :] = jnp.sum(sums[6 * x + c], axis=0, keepdims=True)
            out.append(jnp.where(sub < 6, rows[x], 0.0))
        return out

    def publish(phase, tiles):
        for x in range(4):
            vec[phase - 1, x] = tiles[x]
        vec_edge[phase - 1] = edge_of(tiles)
        send(phase)

    send(0)
    for x in range(4):
        for c in range(3):
            own_geo[x, c] = row_of(first, x, slice(c, c + 1))
        own_geo[x, 3] = THOLE * row_of(first, x, slice(3, 4))

    d0 = [src[x] * pol[x] for x in range(4)]
    field0 = gather_field(0)
    r0 = [src[x] - (d0[x] * ipol[x] - field0[x]) for x in range(4)]
    p0 = [pol[x] * r0[x] for x in range(4)]
    publish(1, p0)
    field1 = gather_field(1)
    y0 = [p0[x] * ipol[x] - field1[x] for x in range(4)]
    q0 = [pol[x] * y0[x] for x in range(4)]
    publish(2, q0)
    field2 = gather_field(2)
    z0 = [q0[x] * ipol[x] - field2[x] for x in range(4)]

    def dot(a, b):
        t = a[0] * b[0]
        for x in range(1, 4):
            t = t + a[x] * b[x]
        return jnp.sum(t, axis=1, keepdims=True)

    set_of = jnp.where(sub < 3, 0, 1)
    four = [dot(r0, p0), dot(p0, y0), dot(y0, q0), dot(q0, z0)]
    mix = jnp.zeros((8, 128), F32)
    for k in range(4):
        mix = jnp.where((lane >> 4) == 2 * k + set_of, four[k], mix)
    part[...] = jnp.sum(mix, axis=0, keepdims=True)

    def plane_copy(i, j, incoming):
        if incoming:
            i, j = -i % 4, -j % 4
        there, back = 4 * i + j, 4 * (-i % 4) + (-j % 4)
        return pltpu.make_async_remote_copy(
            src_ref=part, dst_ref=in_plane.at[back], send_sem=plane_send.at[there], recv_sem=plane_recv.at[back],
            device_id=at(i, j, 0), device_id_type=MESH,
        )

    def line_copy(k, incoming):
        if incoming:
            k = -k % 8
        return pltpu.make_async_remote_copy(
            src_ref=part2, dst_ref=in_line.at[-k % 8], send_sem=line_send.at[k], recv_sem=line_recv.at[-k % 8],
            device_id=at(0, 0, k), device_id_type=MESH,
        )

    others = [ij for ij in PLANE if ij != (0, 0)]
    for i, j in others:
        plane_copy(i, j, False).start()
    total = part[...]
    for i, j in others:
        plane_copy(i, j, True).wait_recv()
        total = total + in_plane[4 * i + j]
    part2[...] = total
    for k in range(1, 8):
        line_copy(k, False).start()
    for k in range(1, 8):
        line_copy(k, True).wait_recv()
        total = total + in_line[k]

    wide = jnp.broadcast_to(total, (8, 128))
    rz0, py, yq, qz = (
        jnp.sum(jnp.where(lane == 16 * (2 * k + set_of), wide, 0.0), axis=1, keepdims=True) for k in range(4)
    )
    gamma0 = rz0 / py
    rz1 = rz0 + gamma0 * (gamma0 * yq - 2.0 * py)
    keep = 1.0 + rz1 / rz0
    gamma1 = rz1 / (keep * (keep * py - 2.0 * gamma0 * yq) + gamma0 * gamma0 * qz)
    by_p = jnp.broadcast_to(gamma0 + gamma1 * keep, (8, 128))
    by_q = jnp.broadcast_to(gamma1 * gamma0, (8, 128))
    slot = lane
    for out, parts in ((dip_out, (d0, 1.0, p0, q0)), (res_out, (r0, -1.0, y0, z0))):
        base, sign, along, across = parts
        tile = [base[x] + sign * (by_p * along[x] - by_q * across[x]) for x in range(4)]
        for b in range(3):
            pick = 32 * ((slot >> 2) & 3) + 3 + 8 * b + (slot >> 4)
            got = [jnp.take_along_axis(tile[x], pick, axis=1) for x in range(4)]
            sx = slot & 3
            whole = jnp.where(sx == 0, got[0], jnp.where(sx == 1, got[1], jnp.where(sx == 2, got[2], got[3])))
            out[0, 0, b] = whole[0:6, :]

    for phase in range(3):
        for n in NEAR:
            copy(phase, n, False).wait_send()
    for i, j in others:
        plane_copy(i, j, False).wait_send()
    for k in range(1, 8):
        line_copy(k, False).wait_send()


def on_device(coords, polar, field, atom_count, pair_list):
    vmem = pl.BlockSpec(memory_space=pltpu.VMEM)
    smem = pl.BlockSpec(memory_space=pltpu.SMEM)
    tile = lambda *n: pltpu.VMEM(tuple(n) + (8, 128), F32)
    dma = lambda *n: pltpu.SemaphoreType.DMA(tuple(n))
    out = jax.ShapeDtypeStruct(field.shape, F32)
    return pl.pallas_call(
        kernel,
        out_shape=(out, out),
        in_specs=[vmem, vmem, vmem, smem, smem],
        out_specs=(vmem, vmem),
        scratch_shapes=[
            tile(3, 2),
            pltpu.VMEM((4, 16, 128), F32),
            pltpu.VMEM((16, 128), F32),
            tile(2, 4),
            tile(2),
            tile(4),
            tile(4),
            tile(4),
            tile(4, 4),
            pltpu.VMEM((8, 4, 16, 128), F32),
            pltpu.VMEM((18, 16, 128), F32),
            tile(2, 8, 4),
            tile(2, 18),
            tile(1),
            tile(10, 7),
            tile(10, 7, 4),
            tile(3, 7),
            tile(10, 7, 6),
            tile(7, 28, 6),
            tile(24),
            tile(4),
            pltpu.VMEM((1, 128), F32),
            pltpu.VMEM((16, 1, 128), F32),
            pltpu.VMEM((1, 128), F32),
            pltpu.VMEM((8, 1, 128), F32),
            dma(3, 26), dma(3, 26), dma(16), dma(16), dma(8), dma(8),
        ],
        compiler_params=pltpu.CompilerParams(collective_id=0, has_side_effects=True),
    )(coords, polar, field, atom_count, pair_list)


def solution(mesh):
    spec = P("gx", "gy", "gz")
    return jax.shard_map(
        on_device, mesh=mesh, in_specs=(spec,) * 5, out_specs=(spec, spec), check_vma=False,
    )
```

profile of v0, /device:TPU:1, one launch (start us, length us, event | category | flops | bytes accessed | tf_op | source)
XLA Modules:
  0.0 47.1 jit_solution(7461936481885223307)
XLA Ops:
  0.6 0.0 copy-start.2
  0.6 0.0 copy-start.1
  0.7 1.3 %copy.8.polar = f32[1,1,3,128]{3,2,1,0:T(4,128)} copy(f32[1,1,3,128]{3,1,2,0:T(1,128)} %param.6) | data formatting | bytes 3072 | tf_op args[1]
  1.9 0.0 copy-done.2
  1.9 0.6 %copy.10.pairs = s32[1,1,3,13]{3,2,1,0:T(4,128)} copy(s32[1,1,3,13]{3,1,2,0:T(1,128)S(1)} %copy-done.2) | data formatting | bytes 312 | tf_op args[4]
  2.5 1.3 %copy.7.coords = f32[1,1,3,3,128]{4,3,2,1,0:T(4,128)} copy(f32[1,1,3,3,128]{4,1,3,2,0:T(1,128)} %param.5) | data formatting | bytes 9216 | tf_op args[0]
  3.8 0.0 copy-done.1
  3.8 0.6 %copy.9.field = f32[1,1,3,6,128]{4,3,2,1,0:T(8,128)} copy(f32[1,1,3,6,128]{4,1,3,2,0:T(1,128)S(1)} %copy-done.1) | data formatting | bytes 18432 | tf_op args[2]
  4.4 40.7 %shard_map.68 = (f32[1,1,3,6,128]{4,3,2,1,0:T(8,128)}, f32[1,1,3,6,128]{4,3,2,1,0:T(8,128)}) custom-call(f32[1,1,3,3,128]{4,3,2,1,0:T(4,128)} %copy.7.coords, f32[1,1,3,128]{3,2,1,0:T(4,128)} %copy.8.polar, f32[1,1,3,6,128]{4,3,2,1,0:T(8,128)} %copy.9.field, s32[1,1,3]{2,1,0:T(1,128)} %count.1, s32[1,1,3,13]{3,2,1,0:T(4,128)} %copy.10.pairs), custom_call_target="tpu_custom_call" | custom-call | tf_op jit(solution)/shard_map/pallas_call | solution.py:432
  45.1 0.0 copy-start
  45.1 1.3 %copy.11 = f32[1,1,3,6,128]{4,1,3,2,0:T(1,128)} copy(f32[1,1,3,6,128]{4,3,2,1,0:T(8,128)} %get-tuple-element.2) | data formatting | bytes 18432 | tf_op jit(solution)/shard_map/pallas_call | solution.py:432
  46.5 0.0 copy-done
  46.5 0.6 %copy.12 = f32[1,1,3,6,128]{4,1,3,2,0:T(1,128)} copy(f32[1,1,3,6,128]{4,3,2,1,0:T(8,128)S(1)} %copy-done) | data formatting | bytes 18432 | tf_op jit(solution)/shard_map/pallas_call | solution.py:432
Async XLA Ops:
  0.6 1.3 %copy-start.2 = (s32[1,1,3,13]{3,1,2,0:T(1,128)S(1)}, s32[1,1,3,13]{3,1,2,0:T(1,128)}, u32[]{:S(2)}) copy-start(s32[1,1,3,13]{3,1,2,0:T(1,128)} %param.9) | copy-start | bytes 472
  0.6 3.2 %copy-start.1 = (f32[1,1,3,6,128]{4,1,3,2,0:T(1,128)S(1)}, f32[1,1,3,6,128]{4,1,3,2,0:T(1,128)}, u32[]{:S(2)}) copy-start(f32[1,1,3,6,128]{4,1,3,2,0:T(1,128)} %param.7) | copy-start | bytes 27652
  45.1 1.3 %copy-start = (f32[1,1,3,6,128]{4,3,2,1,0:T(8,128)S(1)}, f32[1,1,3,6,128]{4,3,2,1,0:T(8,128)}, u32[]{:S(2)}) copy-start(f32[1,1,3,6,128]{4,3,2,1,0:T(8,128)} %get-tuple-element.3) | copy-start | bytes 27652
where the time goes:
time: 47.4 us; the launch traced here: 47.1 us
  Pallas kernels  40.7 us (86%)
  local copies, waits for them, and re-layouts  5.69 us (12%)
  between operations  0.67 us (1%)
    pallas_call x1, Pallas kernels, on_device(): pl.pallas_call(kernel, out_shape=(out, out), in_specs=[vmem, vmem, vmem,...  40.7 us
    unnamed x10, local copies, waits for them, and re-layouts  3.76 us
    pallas_call x2, local copies, waits for them, and re-layouts, on_device(): pl.pallas_call(kernel, out_shape=(out, out), in_specs=[vmem, vmem, vmem,...  1.93 us

commit v1 on v0

--- a/solution.py
+++ b/solution.py
@@ -25,12 +25,6 @@
 EDGE = [n for n in NEAR if n[2] != 0]
 EDGE_ID = {n: i for i, n in enumerate(EDGE)}
 PLANE = [(i, j) for i in range(4) for j in range(4)]
-GREETED = sorted(
-    {(ox % 4, oy % 4, oz % 8) for ox, oy, oz in NEAR}
-    | {(i, j, 0) for i, j in PLANE if (i, j) != (0, 0)}
-    | {(0, 0, k) for k in range(1, 8)}
-)
-
 OWN_COLS = [3, 4, 5, 6]
 FAR_COLS = [0, 1, 2, 7, 8, 9]
 OWN_PAIRS = [(x, c) for c in OWN_COLS for x in range(4)]
@@ -54,7 +48,8 @@
 
 
 def kernel(
-    coords, polar, field, count, pairs, dip_out, res_out,
+    coords_hbm, polar_hbm, field_hbm, count_hbm, pairs_hbm, dip_out, res_out,
+    coords, polar, field, count, pairs, arg_sem,
     packed, first, first_edge, vec, vec_edge, src, pol, ipol, own_geo,
     in_first, in_first_edge, in_vec, in_vec_edge, ext, merged, geo, act, dip, tens, acc, rows,
     part, in_plane, part2, in_line,
@@ -67,9 +62,17 @@
         return {a: lax.rem(me[a] + off[a] % SIZES[a], SIZES[a]) for a in SIZES}
 
     barrier = pltpu.get_barrier_semaphore()
-    for ox, oy, oz in GREETED:
+    for ox, oy, oz in NEAR:
         pl.semaphore_signal(barrier, inc=1, device_id=at(ox, oy, oz), device_id_type=MESH)
 
+    loads = [
+        pltpu.make_async_copy(a, b, arg_sem.at[i])
+        for i, (a, b) in enumerate(
+            ((coords_hbm, coords), (polar_hbm, polar), (field_hbm, field), (count_hbm, count), (pairs_hbm, pairs))
+        )
+    ]
+    for load in loads:
+        load.start()
     lane, sub = lanes(), subs()
     l32 = lane & 31
     zz = l32 - 3
@@ -78,24 +81,27 @@
     valid = (zz >= 0) & (zz < 24)
     dz = 3 - sub
 
+    for load in loads:
+        load.wait()
     for b in range(3):
         slot = lane
-        mask = (slot[0:1] < count[0, 0, b]).astype(F32)
+        mask = (slot[0:1] < count[0, b]).astype(F32)
         packed[b, 0] = jnp.zeros((8, 128), F32)
         packed[b, 1] = jnp.zeros((8, 128), F32)
-        packed[b, 0, 0:6, :] = field[0, 0, b] * mask
-        pol_row = polar[0, 0, b : b + 1, :]
+        for c in range(6):
+            packed[b, 0, c : c + 1, :] = field[6 * b + c] * mask
+        pol_row = polar[b]
         packed[b, 0, 6:7, :] = pol_row
-        s3 = slot[0:3]
-        r3 = sub[0:3]
-        site = jnp.where(r3 == 0, s3 & 3, jnp.where(r3 == 1, (s3 >> 2) & 3, s3 >> 4)).astype(F32) + 0.5
-        packed[b, 1, 0:3, :] = (coords[0, 0, b] - site * HIGH) - site * LOW
+        s1 = slot[0:1]
+        for c, step in enumerate((s1 & 3, (s1 >> 2) & 3, s1 >> 4)):
+            site = step.astype(F32) + 0.5
+            packed[b, 1, c : c + 1, :] = (coords[3 * b + c] - site * HIGH) - site * LOW
         packed[b, 1, 3:4, :] = mask * lax.rsqrt(pol_row)
     bits = []
     for b in range(3):
         word = jnp.int32(0)
         for k in range(13):
-            word = word | (jnp.int32(1) << (pairs[0, 0, b, k] & 31))
+            word = word | (jnp.int32(1) << (pairs[b, 0, k] & 31))
         bits.append(word)
     word = jnp.where(blk <= 0, bits[0], jnp.where(blk == 1, bits[1], bits[2]))
     for x in range(4):
@@ -126,7 +132,7 @@
     first_edge[0:8, :] = edge_of([first[x, 0:8, :] for x in range(4)])
     first_edge[8:16, :] = edge_of([first[x, 8:16, :] for x in range(4)])
 
-    pl.semaphore_wait(barrier, len(GREETED))
+    pl.semaphore_wait(barrier, len(NEAR))
 
     def copy(phase, n, incoming):
         ox, oy, oz = n if not incoming else tuple(-v for v in n)
@@ -412,7 +418,8 @@
             got = [jnp.take_along_axis(tile[x], pick, axis=1) for x in range(4)]
             sx = slot & 3
             whole = jnp.where(sx == 0, got[0], jnp.where(sx == 1, got[1], jnp.where(sx == 2, got[2], got[3])))
-            out[0, 0, b] = whole[0:6, :]
+            for c in range(6):
+                out[6 * b + c] = whole[c : c + 1, :]
 
     for phase in range(3):
         for n in NEAR:
@@ -425,16 +432,21 @@
 
 def on_device(coords, polar, field, atom_count, pair_list):
     vmem = pl.BlockSpec(memory_space=pltpu.VMEM)
-    smem = pl.BlockSpec(memory_space=pltpu.SMEM)
     tile = lambda *n: pltpu.VMEM(tuple(n) + (8, 128), F32)
     dma = lambda *n: pltpu.SemaphoreType.DMA(tuple(n))
-    out = jax.ShapeDtypeStruct(field.shape, F32)
-    return pl.pallas_call(
+    out = jax.ShapeDtypeStruct((18, 1, 128), F32)
+    dipoles, residual = pl.pallas_call(
         kernel,
         out_shape=(out, out),
-        in_specs=[vmem, vmem, vmem, smem, smem],
+        in_specs=[pl.BlockSpec(memory_space=pl.ANY)] * 5,
         out_specs=(vmem, vmem),
         scratch_shapes=[
+            pltpu.VMEM((9, 1, 128), F32),
+            pltpu.VMEM((3, 1, 128), F32),
+            pltpu.VMEM((18, 1, 128), F32),
+            pltpu.SMEM((1, 3), I32),
+            pltpu.SMEM((3, 1, 13), I32),
+            dma(5),
             tile(3, 2),
             pltpu.VMEM((4, 16, 128), F32),
             pltpu.VMEM((16, 128), F32),
@@ -463,7 +475,11 @@
             dma(3, 26), dma(3, 26), dma(16), dma(16), dma(8), dma(8),
         ],
         compiler_params=pltpu.CompilerParams(collective_id=0, has_side_effects=True),
-    )(coords, polar, field, atom_count, pair_list)
+    )(
+        coords.reshape(9, 1, 128), polar.reshape(3, 1, 128), field.reshape(18, 1, 128),
+        atom_count.reshape(1, 3), pair_list.reshape(3, 1, 13),
+    )
+    return dipoles.reshape(field.shape), residual.reshape(field.shape)
 
 
 def solution(mesh):

time: 47.4 us -> 42.4 us (0.89)
  local copies, waits for them, and re-layouts: 5.69 us -> 1.91 us
  Pallas kernels: 40.7 us -> 39.7 us
    pallas_call x2 -> x0, local copies, waits for them, and re-layouts: 1.93 us -> none  [on_device(): pl.pallas_call(kernel, out_shape=(out, out), in_specs=[vmem, vmem, vmem,...]
    unnamed x10 -> x4, local copies, waits for them, and re-layouts: 3.76 us -> 1.91 us
    pallas_call x1, Pallas kernels: 40.7 us -> 39.7 us  [on_device(): pl.pallas_call(kernel, out_shape=(out, out), in_specs=[pl.BlockSpec(memor...]
where the time goes in v1:
time: 42.4 us; the launch traced here: 42.2 us
  Pallas kernels  39.7 us (94%)
  local copies, waits for them, and re-layouts  1.91 us (5%)
  between operations  0.65 us (2%)
    pallas_call x1, Pallas kernels, on_device(): pl.pallas_call(kernel, out_shape=(out, out), in_specs=[pl.BlockSpec(memor...  39.7 us
    unnamed x4, local copies, waits for them, and re-layouts  1.91 us

profile of v1, /device:TPU:1, one launch (start us, length us, event | category | flops | bytes accessed | tf_op | source)
XLA Modules:
  0.0 42.2 jit_solution(8278627939753379247)
XLA Ops:
  0.6 39.7 %shard_map.68 = (f32[18,1,128]{2,1,0:T(1,128)}, f32[18,1,128]{2,1,0:T(1,128)}) custom-call(f32[9,1,128]{2,1,0:T(1,128)} %bitcast.14, f32[3,1,128]{2,1,0:T(1,128)} %bitcast.15, f32[18,1,128]{2,1,0:T(1,128)} %bitcast.11, s32[1,3]{1,0:T(1,128)} %bitcast.17, s32[3,1,13]{2,1,0:T(1,128)} %bitcast.16), custom_call_target="tpu_custom_call" | custom-call | tf_op jit(solution)/shard_map/pallas_call | solution.py:438
  40.3 0.0 copy-start
  40.3 1.3 %copy.11 = f32[1,1,3,6,128]{4,1,3,2,0:T(1,128)} copy(f32[1,1,3,6,128]{4,1,3,2,0:T(1,128)} %bitcast.13) | data formatting | bytes 18432
  41.6 0.0 copy-done
  41.6 0.6 %copy.12 = f32[1,1,3,6,128]{4,1,3,2,0:T(1,128)} copy(f32[1,1,3,6,128]{4,1,3,2,0:T(1,128)S(1)} %bitcast.12) | data formatting | bytes 18432
Async XLA Ops:
  40.3 1.3 %copy-start = (f32[18,1,128]{2,1,0:T(1,128)S(1)}, f32[18,1,128]{2,1,0:T(1,128)}, u32[]{:S(2)}) copy-start(f32[18,1,128]{2,1,0:T(1,128)} %get-tuple-element.5) | copy-start | bytes 27652

commit v2 on v1

--- a/solution.py
+++ b/solution.py
@@ -24,7 +24,19 @@
 FLAT_ID = {n: i for i, n in enumerate(FLAT)}
 EDGE = [n for n in NEAR if n[2] != 0]
 EDGE_ID = {n: i for i, n in enumerate(EDGE)}
-PLANE = [(i, j) for i in range(4) for j in range(4)]
+
+
+def ring(k):
+    return min(k, 4 - k)
+
+
+def stage_group(xs, zs, ys, cores):
+    every = [(x, z, y, c) for x in range(xs) for z in range(zs) for y in range(ys) for c in range(cores)]
+    return sorted(every[1:], key=lambda n: -sum(map(ring, n[:3])))
+
+
+STAGES = [stage_group(1, 1, 1, 2), stage_group(4, 4, 4, 1)]
+
 OWN_COLS = [3, 4, 5, 6]
 FAR_COLS = [0, 1, 2, 7, 8, 9]
 OWN_PAIRS = [(x, c) for c in OWN_COLS for x in range(4)]
@@ -52,9 +64,9 @@
     coords, polar, field, count, pairs, arg_sem,
     packed, first, first_edge, vec, vec_edge, src, pol, ipol, own_geo,
     in_first, in_first_edge, in_vec, in_vec_edge, ext, merged, geo, act, dip, tens, acc, rows,
-    part, in_plane, part2, in_line,
-    send_sem, recv_sem, plane_send, plane_recv, line_send, line_recv,
+    part, send_sem, recv_sem, *sums,
 ):
+    in_sum, sum_send, sum_recv = (sums[i :: 3] for i in range(3))
     me = {a: lax.axis_index(a) for a in SIZES}
 
     def at(ox, oy, oz):
@@ -160,7 +172,7 @@
     ORDER = sorted(NEAR, key=lambda n: (n[0] == 0, -sum(map(abs, n))))
 
     def send(phase):
-        for n in sorted(NEAR, key=lambda n: (n[2] != 0, -sum(map(abs, n)))):
+        for n in sorted(NEAR, key=lambda n: -sum(map(abs, n))):
             copy(phase, n, False).start()
 
     def await_near(phase, far):
@@ -366,38 +378,35 @@
     mix = jnp.zeros((8, 128), F32)
     for k in range(4):
         mix = jnp.where((lane >> 4) == 2 * k + set_of, four[k], mix)
-    part[...] = jnp.sum(mix, axis=0, keepdims=True)
-
-    def plane_copy(i, j, incoming):
+    total = jnp.sum(mix, axis=0, keepdims=True)
+
+    def peer(x, z, y, core):
+        chip = lax.rem((me["gz"] >> 1) + y % 4, 4)
+        return {"gx": lax.rem(me["gx"] + x % 4, 4), "gy": lax.rem(me["gy"] + z % 4, 4),
+                "gz": 2 * chip + ((me["gz"] & 1) ^ core)}
+
+    def sum_copy(stage, n, incoming):
+        x, z, y, core = n
         if incoming:
-            i, j = -i % 4, -j % 4
-        there, back = 4 * i + j, 4 * (-i % 4) + (-j % 4)
+            x, z, y = -x % 4, -z % 4, -y % 4
+        group = STAGES[stage]
+        there, back = group.index((x, z, y, core)), group.index((-x % 4, -z % 4, -y % 4, core))
         return pltpu.make_async_remote_copy(
-            src_ref=part, dst_ref=in_plane.at[back], send_sem=plane_send.at[there], recv_sem=plane_recv.at[back],
-            device_id=at(i, j, 0), device_id_type=MESH,
+            src_ref=part.at[stage], dst_ref=in_sum[stage].at[back],
+            send_sem=sum_send[stage].at[there], recv_sem=sum_recv[stage].at[back],
+            device_id=peer(x, z, y, core), device_id_type=MESH,
         )
 
-    def line_copy(k, incoming):
-        if incoming:
-            k = -k % 8
-        return pltpu.make_async_remote_copy(
-            src_ref=part2, dst_ref=in_line.at[-k % 8], send_sem=line_send.at[k], recv_sem=line_recv.at[-k % 8],
-            device_id=at(0, 0, k), device_id_type=MESH,
-        )
-
-    others = [ij for ij in PLANE if ij != (0, 0)]
-    for i, j in others:
-        plane_copy(i, j, False).start()
-    total = part[...]
-    for i, j in others:
-        plane_copy(i, j, True).wait_recv()
-        total = total + in_plane[4 * i + j]
-    part2[...] = total
-    for k in range(1, 8):
-        line_copy(k, False).start()
-    for k in range(1, 8):
-        line_copy(k, True).wait_recv()
-        total = total + in_line[k]
+    for stage, group in enumerate(STAGES):
+        part[stage] = total
+        for n in group:
+            sum_copy(stage, n, False).start()
+        for n in reversed(group):
+            sum_copy(stage, n, True).wait_recv()
+        lot = [total] + [in_sum[stage][i] for i in range(len(group))]
+        while len(lot) > 1:
+            lot = [lot[i] + lot[i + 1] if i + 1 < len(lot) else lot[i] for i in range(0, len(lot), 2)]
+        total = lot[0]
 
     wide = jnp.broadcast_to(total, (8, 128))
     rz0, py, yq, qz = (
@@ -424,20 +433,29 @@
     for phase in range(3):
         for n in NEAR:
             copy(phase, n, False).wait_send()
-    for i, j in others:
-        plane_copy(i, j, False).wait_send()
-    for k in range(1, 8):
-        line_copy(k, False).wait_send()
+    for stage, group in enumerate(STAGES):
+        for n in group:
+            sum_copy(stage, n, False).wait_send()
+
+
+def put_out(dipoles, residual, dip_out, res_out, sem):
+    copies = [
+        pltpu.make_async_copy(a, b, sem.at[i]) for i, (a, b) in enumerate(((dipoles, dip_out), (residual, res_out)))
+    ]
+    for copy in copies:
+        copy.start()
+    for copy in copies:
+        copy.wait()
 
 
 def on_device(coords, polar, field, atom_count, pair_list):
     vmem = pl.BlockSpec(memory_space=pltpu.VMEM)
     tile = lambda *n: pltpu.VMEM(tuple(n) + (8, 128), F32)
     dma = lambda *n: pltpu.SemaphoreType.DMA(tuple(n))
-    out = jax.ShapeDtypeStruct((18, 1, 128), F32)
+    kept = pltpu.VMEM((18, 1, 128), F32)
     dipoles, residual = pl.pallas_call(
         kernel,
-        out_shape=(out, out),
+        out_shape=(kept, kept),
         in_specs=[pl.BlockSpec(memory_space=pl.ANY)] * 5,
         out_specs=(vmem, vmem),
         scratch_shapes=[
@@ -468,17 +486,20 @@
             tile(7, 28, 6),
             tile(24),
             tile(4),
-            pltpu.VMEM((1, 128), F32),
-            pltpu.VMEM((16, 1, 128), F32),
-            pltpu.VMEM((1, 128), F32),
-            pltpu.VMEM((8, 1, 128), F32),
-            dma(3, 26), dma(3, 26), dma(16), dma(16), dma(8), dma(8),
+            pltpu.VMEM((len(STAGES), 1, 128), F32),
+            dma(3, 26), dma(3, 26),
+            *(s for g in STAGES for s in (pltpu.VMEM((len(g), 1, 128), F32), dma(len(g)), dma(len(g)))),
         ],
         compiler_params=pltpu.CompilerParams(collective_id=0, has_side_effects=True),
     )(
         coords.reshape(9, 1, 128), polar.reshape(3, 1, 128), field.reshape(18, 1, 128),
         atom_count.reshape(1, 3), pair_list.reshape(3, 1, 13),
     )
+    out = jax.ShapeDtypeStruct((18, 1, 128), F32)
+    anywhere = pl.BlockSpec(memory_space=pl.ANY)
+    dipoles, residual = pl.pallas_call(
+        put_out, out_shape=(out, out), in_specs=[vmem] * 2, out_specs=(anywhere,) * 2, scratch_shapes=[dma(2)],
+    )(*(pltpu.with_memory_space_constraint(v, pltpu.VMEM) for v in (dipoles, residual)))
     return dipoles.reshape(field.shape), residual.reshape(field.shape)
 
 

time: 42.4 us -> 39.6 us (0.934)
  local copies, waits for them, and re-layouts: 1.91 us -> 0 us
  Pallas kernels: 39.7 us -> 38.8 us
    unnamed x4 -> x0, local copies, waits for them, and re-layouts: 1.91 us -> none
    pallas_call x1 -> x2, Pallas kernels: 39.7 us -> 38.8 us  [the longest x1 38.2 us: on_device(): pl.pallas_call(kernel, out_shape=(kept, kept), in_specs=[pl.BlockSpec(mem...]
where the time goes in v2:
time: 39.6 us; the launch traced here: 39.4 us
  Pallas kernels  38.8 us (98%)
  between operations  0.64 us (2%)
    pallas_call x1, Pallas kernels, on_device(): pl.pallas_call(kernel, out_shape=(kept, kept), in_specs=[pl.BlockSpec(mem...  38.2 us

profile of v2, /device:TPU:1, one launch (start us, length us, event | category | flops | bytes accessed | tf_op | source)
XLA Modules:
  0.0 39.4 jit_solution(12911882805046694938)
XLA Ops:
  0.6 38.2 %shard_map.68 = (f32[18,1,128]{2,1,0:T(1,128)S(1)}, f32[18,1,128]{2,1,0:T(1,128)S(1)}) custom-call(f32[9,1,128]{2,1,0:T(1,128)} %bitcast.12, f32[3,1,128]{2,1,0:T(1,128)} %bitcast.13, f32[18,1,128]{2,1,0:T(1,128)} %bitcast.11, s32[1,3]{1,0:T(1,128)} %bitcast.15, s32[3,1,13]{2,1,0:T(1,128)} %bitcast.14), custom_call_target="tpu_custom_call" | custom-call | tf_op jit(solution)/shard_map/pallas_call | solution.py:456
  38.8 0.6 %shard_map.69 = (f32[18,1,128]{2,1,0:T(1,128)}, f32[18,1,128]{2,1,0:T(1,128)}) custom-call(f32[18,1,128]{2,1,0:T(1,128)S(1)} %get-tuple-element.6.dipoles, f32[18,1,128]{2,1,0:T(1,128)S(1)} %get-tuple-element.7.residual), custom_call_target="tpu_custom_call" | custom-call | tf_op jit(solution)/shard_map/pallas_call | solution.py:500

commit v3 on v2

--- a/solution.py
+++ b/solution.py
@@ -169,15 +169,13 @@
             device_id=at(ox, oy, oz), device_id_type=MESH,
         )
 
-    ORDER = sorted(NEAR, key=lambda n: (n[0] == 0, -sum(map(abs, n))))
-
     def send(phase):
         for n in sorted(NEAR, key=lambda n: -sum(map(abs, n))):
             copy(phase, n, False).start()
 
-    def await_near(phase, far):
-        for n in ORDER:
-            if (n[0] != 0) == far:
+    def await_from(phase, far, cross):
+        for n in NEAR:
+            if (n[0] != 0, n[1] != 0) == (far, cross):
                 copy(phase, n, True).wait_recv()
 
     def ext_tile(phase, r0, ox, oy, x):
@@ -196,30 +194,36 @@
     def slide(ref, where, shift):
         return pltpu.roll(row_of(ref, *where), shift % 128, 1, stride=1, stride_axis=0)
 
-    def merge_column(phase, r0, col):
+    def merge_column(phase, r0, col, cross):
         ox, x = col_home(col)
-        tiles = {oy: ext_tile(phase, r0, ox, oy, x) for oy in (-1, 0, 1)}
-        for k in range(7):
-            dy = k - 3
-            if dy > 0:
-                tile = jnp.where(group < dy, tiles[1], tiles[0])
-            elif dy < 0:
-                tile = jnp.where(group >= 4 + dy, tiles[-1], tiles[0])
-            else:
-                tile = pltpu.roll(tiles[0], 64, 1)
-            merged[col, k] = tile
-        return tiles
-
-    def merged_shift(k):
-        return -32 * (k - 3) - 3 - (64 if k == 3 else 0)
-
-    def spread_dipoles(phase, cols):
+        if cross:
+            above, below = ext_tile(phase, r0, ox, 1, x), ext_tile(phase, r0, ox, -1, x)
+            for k in range(4, 7):
+                merged[col, k] = jnp.where(group < k - 3, above, below)
+        else:
+            tile = ext_tile(phase, r0, ox, 0, x)
+            merged[col, 0] = pltpu.roll(tile, 64, 1)
+            merged[col, 1] = tile
+
+    def slots(cross):
+        return (4, 7) if cross else (0, 4)
+
+    def slide_slot(col, k, c):
+        turn = k if k < 4 else k - 3
+        return slide(merged, (col, min(k, 1) if k < 4 else k, slice(c, c + 1)), -32 * turn - 3 - (64 if k == 0 else 0))
+
+    def spread_dipoles(phase, cols, cross):
         for col in cols:
-            merge_column(phase, 8 if phase == 0 else 0, col)
+            merge_column(phase, 8 if phase == 0 else 0, col, cross)
         for col in cols:
-            for k in range(7):
+            for k in range(*slots(cross)):
                 for c in range(6):
-                    dip[col, k, c] = slide(merged, (col, k, slice(c, c + 1)), merged_shift(k))
+                    dip[col, k, c] = slide_slot(col, k, c)
+
+    def steps_y(k):
+        if k < 4:
+            return jnp.where(group + k < 4, k, k - 4)
+        return jnp.where(group + k - 3 < 4, k - 7, k - 3)
 
     zp = zz + dz
     oz = (lax.shift_right_arithmetic(zp + 8, 3)) - (lax.shift_right_arithmetic(zz + 8, 3))
@@ -242,45 +246,46 @@
         down = slide(ext, (0, slice(7, 8)), -35)
         return jnp.where(oz == 0, 1.0, jnp.where(oz > 0, up, down))
 
-    def acts(ox):
-        if ox == 0:
-            a = {-1: backward_act(0, -1), 0: self_act(), 1: forward_act(0, 1)}
-        else:
-            a = {oy: (forward_act if ox > 0 else backward_act)(ox, oy) for oy in (-1, 0, 1)}
-        for k in range(7):
-            to = group + (k - 3)
-            tile = jnp.where(to < 0, a[-1], jnp.where(to > 3, a[1], a[0]))
-            act[ox + 1, k] = jnp.where(lawful, tile, 0.0)
-
-    def spread_geometry(cols):
+    def acts(ox, cross):
+        pick = forward_act if ox > 0 else backward_act
+        if not cross:
+            act[ox + 1, 0] = jnp.where(lawful, self_act() if ox == 0 else pick(ox, 0), 0.0)
+            return
+        above = forward_act(0, 1) if ox == 0 else pick(ox, 1)
+        below = backward_act(0, -1) if ox == 0 else pick(ox, -1)
+        for k in range(4, 7):
+            act[ox + 1, k] = jnp.where(lawful, jnp.where(group + k - 3 < 4, below, above), 0.0)
+
+    def spread_geometry(cols, cross):
         for ox in sorted({col_home(c)[0] for c in cols}):
-            acts(ox)
+            acts(ox, cross)
         for col in cols:
-            merge_column(0, 0, col)
+            merge_column(0, 0, col, cross)
         for col in cols:
             ox, x = col_home(col)
-            for k in range(7):
+            for k in range(*slots(cross)):
                 for c in range(4):
-                    tile = slide(merged, (col, k, slice(c, c + 1)), merged_shift(k))
+                    tile = slide_slot(col, k, c)
+                    if c == 1:
+                        tile = tile + SPACING * steps_y(k).astype(F32)
                     if c == 2:
                         tile = tile + SPACING * dz.astype(F32)
                     if c == 3:
-                        tile = tile * act[ox + 1, k]
+                        tile = tile * act[ox + 1, k if cross else 0]
                     geo[col, k, c] = tile
 
-    def tensors(pair_list, base):
+    def tensors(pair_list, base, cross):
         def body(k, carry):
-            shift_y = SPACING * (k - 3).astype(F32)
             for i, (x, col) in enumerate(pair_list):
                 off_x = col - 3 - x
                 dx = geo[col, k, 0] - own_geo[x, 0]
                 if off_x:
                     dx = dx + SPACING * off_x
-                dy = geo[col, k, 1] - own_geo[x, 1] + shift_y
+                dy = geo[col, k, 1] - own_geo[x, 1]
                 dzz = geo[col, k, 2] - own_geo[x, 2]
                 strength = geo[col, k, 3] * own_geo[x, 3]
-                if off_x == 0:
-                    strength = jnp.where((sub == 3) & (k == 3), 0.0, strength)
+                if off_x == 0 and not cross:
+                    strength = jnp.where((sub == 3) & (k == 0), 0.0, strength)
                 r2 = jnp.maximum(dx * dx + dy * dy + dzz * dzz, 1.0)
                 ir = lax.rsqrt(r2)
                 ir2 = ir * ir
@@ -302,11 +307,9 @@
                 tens[k, base + i, 5] = az * dzz - w3
             return carry
 
-        lax.fori_loop(0, 7, body, 0)
-
-    def apply(pair_list, base, start):
-        used = sorted({x for x, _ in pair_list})
-
+        lax.fori_loop(*slots(cross), body, 0)
+
+    def apply(pair_list, base, cross, start):
         def body(k, sums):
             sums = list(sums)
             for i, (x, col) in enumerate(pair_list):
@@ -319,23 +322,23 @@
                     sums[o + 2] = sums[o + 2] + (t[2] * vx + t[4] * vy + t[5] * vz)
             return tuple(sums)
 
-        return lax.fori_loop(0, 7, body, start)
+        return lax.fori_loop(*slots(cross), body, start)
 
     def gather_field(phase):
-        await_near(phase, False)
-        if phase == 0:
-            spread_geometry(OWN_COLS)
-            tensors(OWN_PAIRS, 0)
-        spread_dipoles(phase, OWN_COLS)
-        sums = apply(OWN_PAIRS, 0, tuple(jnp.zeros((8, 128), F32) for _ in range(24)))
-        for i in range(24):
-            acc[i] = sums[i]
-        await_near(phase, True)
-        if phase == 0:
-            spread_geometry(FAR_COLS)
-            tensors(FAR_PAIRS, 16)
-        spread_dipoles(phase, FAR_COLS)
-        sums = apply(FAR_PAIRS, 16, tuple(acc[i] for i in range(24)))
+        sums = tuple(jnp.zeros((8, 128), F32) for _ in range(24))
+        for far, cross in ((False, False), (False, True), (True, False), (True, True)):
+            cols, pair_list, base = (FAR_COLS, FAR_PAIRS, 16) if far else (OWN_COLS, OWN_PAIRS, 0)
+            await_from(phase, far, cross)
+            if phase == 0:
+                spread_geometry(cols, cross)
+                tensors(pair_list, base, cross)
+            spread_dipoles(phase, cols, cross)
+            if far or cross:
+                sums = tuple(acc[i] for i in range(24))
+            sums = apply(pair_list, base, cross, sums)
+            if not (far and cross):
+                for i in range(24):
+                    acc[i] = sums[i]
         out = []
         for x in range(4):
             for c in range(6):

time: 39.6 us -> 38.2 us (0.965)
  Pallas kernels: 38.8 us -> 37.4 us
    pallas_call x1, Pallas kernels: 38.2 us -> 36.7 us  [on_device(): pl.pallas_call(kernel, out_shape=(kept, kept), in_specs=[pl.BlockSpec(mem...]
where the time goes in v3:
time: 38.2 us; the launch traced here: 38 us
  Pallas kernels  37.4 us (98%)
  between operations  0.64 us (2%)
    pallas_call x1, Pallas kernels, on_device(): pl.pallas_call(kernel, out_shape=(kept, kept), in_specs=[pl.BlockSpec(mem...  36.7 us

profile of v3, /device:TPU:1, one launch (start us, length us, event | category | flops | bytes accessed | tf_op | source)
XLA Modules:
  0.0 38.0 jit_solution(10478768902320542346)
XLA Ops:
  0.6 36.7 %shard_map.68 = (f32[18,1,128]{2,1,0:T(1,128)S(1)}, f32[18,1,128]{2,1,0:T(1,128)S(1)}) custom-call(f32[9,1,128]{2,1,0:T(1,128)} %bitcast.12, f32[3,1,128]{2,1,0:T(1,128)} %bitcast.13, f32[18,1,128]{2,1,0:T(1,128)} %bitcast.11, s32[1,3]{1,0:T(1,128)} %bitcast.15, s32[3,1,13]{2,1,0:T(1,128)} %bitcast.14), custom_call_target="tpu_custom_call" | custom-call | tf_op jit(solution)/shard_map/pallas_call | solution.py:459
  37.4 0.6 %shard_map.69 = (f32[18,1,128]{2,1,0:T(1,128)}, f32[18,1,128]{2,1,0:T(1,128)}) custom-call(f32[18,1,128]{2,1,0:T(1,128)S(1)} %get-tuple-element.6.dipoles, f32[18,1,128]{2,1,0:T(1,128)S(1)} %get-tuple-element.7.residual), custom_call_target="tpu_custom_call" | custom-call | tf_op jit(solution)/shard_map/pallas_call | solution.py:503

commit v4 on v3

--- a/solution.py
+++ b/solution.py
@@ -64,7 +64,7 @@
     coords, polar, field, count, pairs, arg_sem,
     packed, first, first_edge, vec, vec_edge, src, pol, ipol, own_geo,
     in_first, in_first_edge, in_vec, in_vec_edge, ext, merged, geo, act, dip, tens, acc, rows,
-    part, send_sem, recv_sem, *sums,
+    part, home, send_sem, recv_sem, *sums,
 ):
     in_sum, sum_send, sum_recv = (sums[i :: 3] for i in range(3))
     me = {a: lax.axis_index(a) for a in SIZES}
@@ -363,25 +363,29 @@
     r0 = [src[x] - (d0[x] * ipol[x] - field0[x]) for x in range(4)]
     p0 = [pol[x] * r0[x] for x in range(4)]
     publish(1, p0)
-    field1 = gather_field(1)
-    y0 = [p0[x] * ipol[x] - field1[x] for x in range(4)]
-    q0 = [pol[x] * y0[x] for x in range(4)]
-    publish(2, q0)
-    field2 = gather_field(2)
-    z0 = [q0[x] * ipol[x] - field2[x] for x in range(4)]
-
-    def dot(a, b):
+    t0 = gather_field(1)
+    s0 = [pol[x] * t0[x] for x in range(4)]
+    publish(2, s0)
+    set_of = jnp.where(sub < 3, 0, 1)
+
+    def with_dot(mix, k, a, b):
         t = a[0] * b[0]
         for x in range(1, 4):
             t = t + a[x] * b[x]
-        return jnp.sum(t, axis=1, keepdims=True)
-
-    set_of = jnp.where(sub < 3, 0, 1)
-    four = [dot(r0, p0), dot(p0, y0), dot(y0, q0), dot(q0, z0)]
+        return jnp.where((lane >> 4) == 2 * k + set_of, jnp.sum(t, axis=1, keepdims=True), mix)
+
     mix = jnp.zeros((8, 128), F32)
-    for k in range(4):
-        mix = jnp.where((lane >> 4) == 2 * k + set_of, four[k], mix)
-    total = jnp.sum(mix, axis=0, keepdims=True)
+    for k, (a, b) in enumerate(((r0, p0), (p0, t0), (t0, s0))):
+        mix = with_dot(mix, k, a, b)
+    field2 = gather_field(2)
+    w0 = [s0[x] * ipol[x] - field2[x] for x in range(4)]
+    total = jnp.sum(with_dot(mix, 3, s0, w0), axis=0, keepdims=True)
+
+    def in_slot_order(tiles, b):
+        pick = 32 * ((lane >> 2) & 3) + 3 + 8 * b + (lane >> 4)
+        got = [jnp.take_along_axis(tiles[x], pick, axis=1) for x in range(4)]
+        at_x = lane & 3
+        return jnp.where(at_x == 0, got[0], jnp.where(at_x == 1, got[1], jnp.where(at_x == 2, got[2], got[3])))
 
     def peer(x, z, y, core):
         chip = lax.rem((me["gz"] >> 1) + y % 4, 4)
@@ -404,6 +408,10 @@
         part[stage] = total
         for n in group:
             sum_copy(stage, n, False).start()
+        if stage == len(STAGES) - 1:
+            for b in range(3):
+                for i, tiles in enumerate((d0, p0, s0, r0, t0, w0)):
+                    home[b, i] = in_slot_order(tiles, b)
         for n in reversed(group):
             sum_copy(stage, n, True).wait_recv()
         lot = [total] + [in_sum[stage][i] for i in range(len(group))]
@@ -412,26 +420,23 @@
         total = lot[0]
 
     wide = jnp.broadcast_to(total, (8, 128))
-    rz0, py, yq, qz = (
+    rz0, pt, ts, sw = (
         jnp.sum(jnp.where(lane == 16 * (2 * k + set_of), wide, 0.0), axis=1, keepdims=True) for k in range(4)
     )
-    gamma0 = rz0 / py
-    rz1 = rz0 + gamma0 * (gamma0 * yq - 2.0 * py)
-    keep = 1.0 + rz1 / rz0
-    gamma1 = rz1 / (keep * (keep * py - 2.0 * gamma0 * yq) + gamma0 * gamma0 * qz)
+    over = pt / (rz0 - pt)
+    gamma0 = 1.0 + over
+    rz1 = over * (over * rz0 - 2.0 * gamma0 * pt) + gamma0 * gamma0 * ts
+    keep = rz1 / rz0 - over
+    curve = keep * (keep * (rz0 - pt) + 2.0 * gamma0 * (pt - ts)) + gamma0 * gamma0 * sw
+    gamma1 = rz1 / curve
     by_p = jnp.broadcast_to(gamma0 + gamma1 * keep, (8, 128))
-    by_q = jnp.broadcast_to(gamma1 * gamma0, (8, 128))
-    slot = lane
-    for out, parts in ((dip_out, (d0, 1.0, p0, q0)), (res_out, (r0, -1.0, y0, z0))):
-        base, sign, along, across = parts
-        tile = [base[x] + sign * (by_p * along[x] - by_q * across[x]) for x in range(4)]
-        for b in range(3):
-            pick = 32 * ((slot >> 2) & 3) + 3 + 8 * b + (slot >> 4)
-            got = [jnp.take_along_axis(tile[x], pick, axis=1) for x in range(4)]
-            sx = slot & 3
-            whole = jnp.where(sx == 0, got[0], jnp.where(sx == 1, got[1], jnp.where(sx == 2, got[2], got[3])))
+    by_s = jnp.broadcast_to(gamma1 * gamma0, (8, 128))
+    by_r = jnp.broadcast_to(over + gamma1 * keep, (8, 128))
+    for b in range(3):
+        d, p, s, r, t, w = (home[b, i] for i in range(6))
+        for out, slots in ((dip_out, d + by_p * p + by_s * s), (res_out, by_p * t - by_r * r - by_s * w)):
             for c in range(6):
-                out[6 * b + c] = whole[c : c + 1, :]
+                out[6 * b + c] = slots[c : c + 1, :]
 
     for phase in range(3):
         for n in NEAR:
@@ -490,6 +495,7 @@
             tile(24),
             tile(4),
             pltpu.VMEM((len(STAGES), 1, 128), F32),
+            tile(3, 6),
             dma(3, 26), dma(3, 26),
             *(s for g in STAGES for s in (pltpu.VMEM((len(g), 1, 128), F32), dma(len(g)), dma(len(g)))),
         ],

time: 38.2 us -> 38.1 us (level)
  no operation moved by 1% of the time
where the time goes in v4:
time: 38.1 us; the launch traced here: 37.9 us
  Pallas kernels  37.2 us (98%)
  between operations  0.64 us (2%)
    pallas_call x1, Pallas kernels, on_device(): pl.pallas_call(kernel, out_shape=(kept, kept), in_specs=[pl.BlockSpec(mem...  36.6 us

profile of v4, /device:TPU:1, one launch (start us, length us, event | category | flops | bytes accessed | tf_op | source)
XLA Modules:
  0.0 37.9 jit_solution(3014046636624210261)
XLA Ops:
  0.6 36.6 %shard_map.68 = (f32[18,1,128]{2,1,0:T(1,128)S(1)}, f32[18,1,128]{2,1,0:T(1,128)S(1)}) custom-call(f32[9,1,128]{2,1,0:T(1,128)} %bitcast.12, f32[3,1,128]{2,1,0:T(1,128)} %bitcast.13, f32[18,1,128]{2,1,0:T(1,128)} %bitcast.11, s32[1,3]{1,0:T(1,128)} %bitcast.15, s32[3,1,13]{2,1,0:T(1,128)} %bitcast.14), custom_call_target="tpu_custom_call" | custom-call | tf_op jit(solution)/shard_map/pallas_call | solution.py:464
  37.3 0.6 %shard_map.69 = (f32[18,1,128]{2,1,0:T(1,128)}, f32[18,1,128]{2,1,0:T(1,128)}) custom-call(f32[18,1,128]{2,1,0:T(1,128)S(1)} %get-tuple-element.6.dipoles, f32[18,1,128]{2,1,0:T(1,128)S(1)} %get-tuple-element.7.residual), custom_call_target="tpu_custom_call" | custom-call | tf_op jit(solution)/shard_map/pallas_call | solution.py:509

commit v5 on v4

--- a/solution.py
+++ b/solution.py
@@ -307,7 +307,7 @@
                 tens[k, base + i, 5] = az * dzz - w3
             return carry
 
-        lax.fori_loop(*slots(cross), body, 0)
+        lax.fori_loop(*slots(cross), body, 0, unroll=True)
 
     def apply(pair_list, base, cross, start):
         def body(k, sums):
@@ -322,7 +322,7 @@
                     sums[o + 2] = sums[o + 2] + (t[2] * vx + t[4] * vy + t[5] * vz)
             return tuple(sums)
 
-        return lax.fori_loop(*slots(cross), body, start)
+        return lax.fori_loop(*slots(cross), body, start, unroll=True)
 
     def gather_field(phase):
         sums = tuple(jnp.zeros((8, 128), F32) for _ in range(24))
@@ -412,6 +412,12 @@
             for b in range(3):
                 for i, tiles in enumerate((d0, p0, s0, r0, t0, w0)):
                     home[b, i] = in_slot_order(tiles, b)
+            for phase in range(3):
+                for n in NEAR:
+                    copy(phase, n, False).wait_send()
+            for done in range(stage + 1):
+                for n in STAGES[done]:
+                    sum_copy(done, n, False).wait_send()
         for n in reversed(group):
             sum_copy(stage, n, True).wait_recv()
         lot = [total] + [in_sum[stage][i] for i in range(len(group))]
@@ -437,13 +443,6 @@
         for out, slots in ((dip_out, d + by_p * p + by_s * s), (res_out, by_p * t - by_r * r - by_s * w)):
             for c in range(6):
                 out[6 * b + c] = slots[c : c + 1, :]
-
-    for phase in range(3):
-        for n in NEAR:
-            copy(phase, n, False).wait_send()
-    for stage, group in enumerate(STAGES):
-        for n in group:
-            sum_copy(stage, n, False).wait_send()
 
 
 def put_out(dipoles, residual, dip_out, res_out, sem):

time: 38.1 us -> 36.3 us (0.953)
  Pallas kernels: 37.2 us -> 35.5 us
    pallas_call x1, Pallas kernels: 36.6 us -> 34.9 us  [on_device(): pl.pallas_call(kernel, out_shape=(kept, kept), in_specs=[pl.BlockSpec(mem...]
where the time goes in v5:
time: 36.3 us; the launch traced here: 36.2 us
  Pallas kernels  35.5 us (98%)
  between operations  0.64 us (2%)
    pallas_call x1, Pallas kernels, on_device(): pl.pallas_call(kernel, out_shape=(kept, kept), in_specs=[pl.BlockSpec(mem...  34.9 us

profile of v5, /device:TPU:1, one launch (start us, length us, event | category | flops | bytes accessed | tf_op | source)
XLA Modules:
  0.0 36.2 jit_solution(6390591926068305716)
XLA Ops:
  0.6 34.9 %shard_map.68 = (f32[18,1,128]{2,1,0:T(1,128)S(1)}, f32[18,1,128]{2,1,0:T(1,128)S(1)}) custom-call(f32[9,1,128]{2,1,0:T(1,128)} %bitcast.12, f32[3,1,128]{2,1,0:T(1,128)} %bitcast.13, f32[18,1,128]{2,1,0:T(1,128)} %bitcast.11, s32[1,3]{1,0:T(1,128)} %bitcast.15, s32[3,1,13]{2,1,0:T(1,128)} %bitcast.14), custom_call_target="tpu_custom_call" | custom-call | tf_op jit(solution)/shard_map/pallas_call | solution.py:463
  35.6 0.6 %shard_map.69 = (f32[18,1,128]{2,1,0:T(1,128)}, f32[18,1,128]{2,1,0:T(1,128)}) custom-call(f32[18,1,128]{2,1,0:T(1,128)S(1)} %get-tuple-element.6.dipoles, f32[18,1,128]{2,1,0:T(1,128)S(1)} %get-tuple-element.7.residual), custom_call_target="tpu_custom_call" | custom-call | tf_op jit(solution)/shard_map/pallas_call | solution.py:508

commit v6 on v5

--- a/solution.py
+++ b/solution.py
@@ -63,7 +63,7 @@
     coords_hbm, polar_hbm, field_hbm, count_hbm, pairs_hbm, dip_out, res_out,
     coords, polar, field, count, pairs, arg_sem,
     packed, first, first_edge, vec, vec_edge, src, pol, ipol, own_geo,
-    in_first, in_first_edge, in_vec, in_vec_edge, ext, merged, geo, act, dip, tens, acc, rows,
+    in_first, in_first_edge, in_vec, in_vec_edge, ext, merged, geo, act, dip, tens, rows,
     part, home, send_sem, recv_sem, *sums,
 ):
     in_sum, sum_send, sum_recv = (sums[i :: 3] for i in range(3))
@@ -72,10 +72,6 @@
     def at(ox, oy, oz):
         off = {"gx": ox, "gy": oy, "gz": oz}
         return {a: lax.rem(me[a] + off[a] % SIZES[a], SIZES[a]) for a in SIZES}
-
-    barrier = pltpu.get_barrier_semaphore()
-    for ox, oy, oz in NEAR:
-        pl.semaphore_signal(barrier, inc=1, device_id=at(ox, oy, oz), device_id_type=MESH)
 
     loads = [
         pltpu.make_async_copy(a, b, arg_sem.at[i])
@@ -85,6 +81,10 @@
     ]
     for load in loads:
         load.start()
+    barrier = pltpu.get_barrier_semaphore()
+    for ox, oy, oz in NEAR:
+        pl.semaphore_signal(barrier, inc=1, device_id=at(ox, oy, oz), device_id_type=MESH)
+
     lane, sub = lanes(), subs()
     l32 = lane & 31
     zz = l32 - 3
@@ -333,12 +333,7 @@
                 spread_geometry(cols, cross)
                 tensors(pair_list, base, cross)
             spread_dipoles(phase, cols, cross)
-            if far or cross:
-                sums = tuple(acc[i] for i in range(24))
             sums = apply(pair_list, base, cross, sums)
-            if not (far and cross):
-                for i in range(24):
-                    acc[i] = sums[i]
         out = []
         for x in range(4):
             for c in range(6):
@@ -491,7 +486,6 @@
             tile(3, 7),
             tile(10, 7, 6),
             tile(7, 28, 6),
-            tile(24),
             tile(4),
             pltpu.VMEM((len(STAGES), 1, 128), F32),
             tile(3, 6),

time: 36.3 us -> 36.3 us (level)
  no operation moved by 1% of the time
where the time goes in v6:
time: 36.3 us; the launch traced here: 36.2 us
  Pallas kernels  35.5 us (98%)
  between operations  0.64 us (2%)
    pallas_call x1, Pallas kernels, on_device(): pl.pallas_call(kernel, out_shape=(kept, kept), in_specs=[pl.BlockSpec(mem...  34.9 us

profile of v6, /device:TPU:1, one launch (start us, length us, event | category | flops | bytes accessed | tf_op | source)
XLA Modules:
  0.0 36.2 jit_solution(13682291375852184453)
XLA Ops:
  0.6 34.9 %shard_map.68 = (f32[18,1,128]{2,1,0:T(1,128)S(1)}, f32[18,1,128]{2,1,0:T(1,128)S(1)}) custom-call(f32[9,1,128]{2,1,0:T(1,128)} %bitcast.12, f32[3,1,128]{2,1,0:T(1,128)} %bitcast.13, f32[18,1,128]{2,1,0:T(1,128)} %bitcast.11, s32[1,3]{1,0:T(1,128)} %bitcast.15, s32[3,1,13]{2,1,0:T(1,128)} %bitcast.14), custom_call_target="tpu_custom_call" | custom-call | tf_op jit(solution)/shard_map/pallas_call | solution.py:458
  35.6 0.6 %shard_map.69 = (f32[18,1,128]{2,1,0:T(1,128)}, f32[18,1,128]{2,1,0:T(1,128)}) custom-call(f32[18,1,128]{2,1,0:T(1,128)S(1)} %get-tuple-element.6.dipoles, f32[18,1,128]{2,1,0:T(1,128)S(1)} %get-tuple-element.7.residual), custom_call_target="tpu_custom_call" | custom-call | tf_op jit(solution)/shard_map/pallas_call | solution.py:502

commit v7 on v5

--- a/solution.py
+++ b/solution.py
@@ -199,26 +199,26 @@
         if cross:
             above, below = ext_tile(phase, r0, ox, 1, x), ext_tile(phase, r0, ox, -1, x)
             for k in range(4, 7):
-                merged[col, k] = jnp.where(group < k - 3, above, below)
+                merged[r0 // 8 if phase == 0 else 0, col, k] = jnp.where(group < k - 3, above, below)
         else:
             tile = ext_tile(phase, r0, ox, 0, x)
-            merged[col, 0] = pltpu.roll(tile, 64, 1)
-            merged[col, 1] = tile
+            merged[r0 // 8 if phase == 0 else 0, col, 0] = pltpu.roll(tile, 64, 1)
+            merged[r0 // 8 if phase == 0 else 0, col, 1] = tile
 
     def slots(cross):
         return (4, 7) if cross else (0, 4)
 
-    def slide_slot(col, k, c):
+    def slide_slot(which, col, k, c):
         turn = k if k < 4 else k - 3
-        return slide(merged, (col, min(k, 1) if k < 4 else k, slice(c, c + 1)), -32 * turn - 3 - (64 if k == 0 else 0))
+        return slide(merged, (which, col, min(k, 1) if k < 4 else k, slice(c, c + 1)), -32 * turn - 3 - (64 if k == 0 else 0))
 
     def spread_dipoles(phase, cols, cross):
         for col in cols:
             merge_column(phase, 8 if phase == 0 else 0, col, cross)
-        for col in cols:
-            for k in range(*slots(cross)):
+        for k in range(*slots(cross)):
+            for col in cols:
                 for c in range(6):
-                    dip[col, k, c] = slide_slot(col, k, c)
+                    dip[col, k, c] = slide_slot(1 if phase == 0 else 0, col, k, c)
 
     def steps_y(k):
         if k < 4:
@@ -261,11 +261,11 @@
             acts(ox, cross)
         for col in cols:
             merge_column(0, 0, col, cross)
-        for col in cols:
-            ox, x = col_home(col)
-            for k in range(*slots(cross)):
+        for k in range(*slots(cross)):
+            for col in cols:
+                ox, x = col_home(col)
                 for c in range(4):
-                    tile = slide_slot(col, k, c)
+                    tile = slide_slot(0, col, k, c)
                     if c == 1:
                         tile = tile + SPACING * steps_y(k).astype(F32)
                     if c == 2:
@@ -331,8 +331,9 @@
             await_from(phase, far, cross)
             if phase == 0:
                 spread_geometry(cols, cross)
+            spread_dipoles(phase, cols, cross)
+            if phase == 0:
                 tensors(pair_list, base, cross)
-            spread_dipoles(phase, cols, cross)
             if far or cross:
                 sums = tuple(acc[i] for i in range(24))
             sums = apply(pair_list, base, cross, sums)
@@ -486,7 +487,7 @@
             tile(2, 8, 4),
             tile(2, 18),
             tile(1),
-            tile(10, 7),
+            tile(2, 10, 7),
             tile(10, 7, 4),
             tile(3, 7),
             tile(10, 7, 6),

time: 36.3 us -> 36.3 us (level)
  no operation moved by 1% of the time
where the time goes in v7:
time: 36.3 us; the launch traced here: 36.2 us
  Pallas kernels  35.5 us (98%)
  between operations  0.64 us (2%)
    pallas_call x1, Pallas kernels, on_device(): pl.pallas_call(kernel, out_shape=(kept, kept), in_specs=[pl.BlockSpec(mem...  34.9 us

profile of v7, /device:TPU:1, one launch (start us, length us, event | category | flops | bytes accessed | tf_op | source)
XLA Modules:
  0.0 36.2 jit_solution(14149529438738811421)
XLA Ops:
  0.6 34.9 %shard_map.68 = (f32[18,1,128]{2,1,0:T(1,128)S(1)}, f32[18,1,128]{2,1,0:T(1,128)S(1)}) custom-call(f32[9,1,128]{2,1,0:T(1,128)} %bitcast.12, f32[3,1,128]{2,1,0:T(1,128)} %bitcast.13, f32[18,1,128]{2,1,0:T(1,128)} %bitcast.11, s32[1,3]{1,0:T(1,128)} %bitcast.15, s32[3,1,13]{2,1,0:T(1,128)} %bitcast.14), custom_call_target="tpu_custom_call" | custom-call | tf_op jit(solution)/shard_map/pallas_call | solution.py:464
  35.6 0.6 %shard_map.69 = (f32[18,1,128]{2,1,0:T(1,128)}, f32[18,1,128]{2,1,0:T(1,128)}) custom-call(f32[18,1,128]{2,1,0:T(1,128)S(1)} %get-tuple-element.6.dipoles, f32[18,1,128]{2,1,0:T(1,128)S(1)} %get-tuple-element.7.residual), custom_call_target="tpu_custom_call" | custom-call | tf_op jit(solution)/shard_map/pallas_call | solution.py:509
